TPU v7x, 32 devices: a whole 2x2x4 slice. The times are simulated.
32 devices in a mesh: rows: 8 (over z, y), model: 4 (over x, core).
Axes of the slice: x: 2, y: 2, z: 4, core: 2. Of those that a mesh axis runs over, the one named last changes fastest.
Arguments:
- w_query: float32 [4096, 4096], P('rows', 'model'), may hold values from -0.125 to 0.125
- first_query: float32 [4096, 4096], P('rows', 'model'), may hold values from -6 to 6
- second_query: float32 [4096, 4096], P('rows', 'model'), may hold values from 0.1 to 10
- w_key: float32 [4096, 1024], P('rows', 'model'), may hold values from -0.125 to 0.125
- first_key: float32 [4096, 1024], P('rows', 'model'), may hold values from -6 to 6
- second_key: float32 [4096, 1024], P('rows', 'model'), may hold values from 0.1 to 10
- w_value: float32 [4096, 1024], P('rows', 'model'), may hold values from -0.125 to 0.125
- first_value: float32 [4096, 1024], P('rows', 'model'), may hold values from -6 to 6
- second_value: float32 [4096, 1024], P('rows', 'model'), may hold values from 0.1 to 10
- norm_train: float32 [4096], P(('rows', 'model')), may hold values from 0.25 to 1.75
- norm_step: float32 [4096], P(('rows', 'model')), may hold values from -0.3 to 0.3
Outputs:
- final_query: bfloat16 [4096, 4096], P(None, 'model')
- final_key: bfloat16 [4096, 1024], P(None, 'model')
- final_value: bfloat16 [4096, 1024], P(None, 'model')
- column_query: float32 [4096], P('model')
- column_key: float32 [1024], P('model')
- column_value: float32 [1024], P('model')
- serve_norm: bfloat16 [4096], replicated
- result_query: float32 [4096, 4096], P('rows', 'model')
- result_key: float32 [4096, 1024], P('rows', 'model')
- result_value: float32 [4096, 1024], P('rows', 'model')
All inputs are finite; a program needn't handle non-finite values. Where the computation divides by a largest or mean magnitude, that divisor is 1e-20 or more.
Results may differ from a plain program's by a relative error of at most 0.0004.
Values may be sent and summed in bfloat16 or wider, within the bound.
A program may use at most 64 MiB of HBM per device.

v0:
```python
import functools

import jax
import jax.numpy as jnp
from jax import lax
from jax.experimental import pallas as pl
from jax.experimental.pallas import tpu as pltpu
from jax.sharding import PartitionSpec as P

learn_rate = 0.01
decay_rate = 0.05
tiny_value = 1e-08

MESH = pl.DeviceIdType.MESH
SIDE = 2
TILE = 32
PIECES = 4


def adam(w, first, second):
    return w - learn_rate * (first / (jnp.sqrt(second) + tiny_value) + decay_rate * w)


def plain(d_model, arrays):
    *weights, norm_train, norm_step = arrays
    results = [adam(*weights[3 * i : 3 * i + 3]) for i in range(3)]
    totals = lax.psum(tuple(jnp.sum(jnp.abs(r), axis=0) for r in results), "rows")
    columns = [t / d_model for t in totals]
    finals = [
        lax.all_gather((r / c).astype(jnp.bfloat16), "rows", axis=0, tiled=True)
        for r, c in zip(results, columns)
    ]
    serve = lax.all_gather(
        (norm_train + norm_step).astype(jnp.bfloat16), ("rows", "model"), axis=0, tiled=True
    )
    return (*finals, *columns, serve, *results)


def kernel(
    n_rows, n_model, blocks, d_model,
    *refs,
):
    ins, refs = refs[:9], refs[9:]
    nt_ref, ns_ref = refs[:2]
    finals, cols, norm_out, results = refs[2:5], refs[5:8], refs[8], refs[9:12]
    bufs = refs[12:21]
    (sums, gains, in_sem, sum_send, sum_recv, gain_send, gain_recv,
     up_send, down_send, side_send, line_recv, side_recv) = refs[21:]

    line = n_rows // SIDE
    me = lax.axis_index("rows")
    col = lax.axis_index("model")
    z, y = me // SIDE, me % SIDE
    other = 1 - y
    share = bufs[0].shape[0]
    nb = len(blocks)
    lead = nb - 1

    loads = []
    for b, (a, start, width) in enumerate(blocks):
        for k in range(3):
            where = (slice(None), pl.ds(start, width))
            c = pltpu.make_async_copy(
                ins[3 * a + k].at[where], bufs[3 * a + k].at[where], in_sem.at[b, k]
            )
            c.start()
            loads.append(c)

    barrier = pltpu.get_barrier_semaphore()
    for k in range(1, n_rows):
        pl.semaphore_signal(
            barrier, inc=1, device_id={"rows": lax.rem(me + k, n_rows)}, device_id_type=MESH
        )
    for k in range(1, n_model):
        pl.semaphore_signal(
            barrier, inc=1, device_id={"model": lax.rem(col + k, n_model)}, device_id_type=MESH
        )
    gains[me, col] = nt_ref[...] + ns_ref[...]

    def step(b):
        a, start, width = blocks[b]
        for k in range(3):
            loads[3 * b + k].wait()

        def one(i, acc):
            rows = pl.ds(pl.multiple_of(i * TILE, TILE), TILE)
            where = (rows, pl.ds(start, width))
            r = adam(*(bufs[3 * a + k][where] for k in range(3)))
            results[a][where] = r
            m = jnp.abs(r).reshape(TILE // 8, 8, width)
            return acc + jnp.sum(m, axis=0)

        acc = lax.fori_loop(0, share // TILE, one, jnp.zeros((8, width), jnp.float32))
        sums[b, me] = jnp.sum(acc, axis=0, keepdims=True)

    def sum_copy(b, k):
        return pltpu.make_async_remote_copy(
            src_ref=sums.at[b, me],
            dst_ref=sums.at[b, me],
            send_sem=sum_send.at[b, k],
            recv_sem=sum_recv.at[b, k],
            device_id={"rows": lax.rem(me + k, n_rows)},
            device_id_type=MESH,
        )

    def wait_sum(b, k):
        who = lax.rem(me + n_rows - k, n_rows)
        pltpu.make_async_remote_copy(
            src_ref=sums.at[b, who],
            dst_ref=sums.at[b, who],
            send_sem=sum_send.at[b, k],
            recv_sem=sum_recv.at[b, k],
            device_id={"rows": lax.rem(me + k, n_rows)},
            device_id_type=MESH,
        ).wait_recv()

    def place(j, owner):
        a, start, width = blocks[j]
        rows = pl.ds(pl.multiple_of(owner * share, share), share)
        return finals[a].at[rows, pl.ds(start, width)]

    def to_line(zs, j, up):
        owner = zs * SIDE + (other if j == nb else y)
        part = place(min(j, lead), owner)
        return pltpu.make_async_remote_copy(
            src_ref=part,
            dst_ref=part,
            send_sem=(up_send if up else down_send).at[zs, j],
            recv_sem=line_recv.at[zs, j],
            device_id={"rows": me + (SIDE if up else -SIDE)},
            device_id_type=MESH,
        )

    def to_side(zs, j, mine=True):
        part = place(j, zs * SIDE + (y if mine else other))
        return pltpu.make_async_remote_copy(
            src_ref=part,
            dst_ref=part,
            send_sem=side_send.at[zs, j],
            recv_sem=side_recv.at[zs, j],
            device_id={"rows": z * SIDE + other},
            device_id_type=MESH,
        )

    def both_ways(zs, j):
        @pl.when(z > 0)
        def _():
            to_line(zs, j, False).start()

        @pl.when(z < line - 1)
        def _():
            to_line(zs, j, True).start()

    def gain_model(k):
        return pltpu.make_async_remote_copy(
            src_ref=gains.at[me, col],
            dst_ref=gains.at[me, col],
            send_sem=gain_send.at[k],
            recv_sem=gain_recv.at[k],
            device_id={"model": lax.rem(col + k, n_model)},
            device_id_type=MESH,
        )

    def gain_rows(k, who):
        return pltpu.make_async_remote_copy(
            src_ref=gains.at[who],
            dst_ref=gains.at[who],
            send_sem=gain_send.at[n_model + k],
            recv_sem=gain_recv.at[n_model + k],
            device_id={"rows": lax.rem(me + k, n_rows)},
            device_id_type=MESH,
        )

    order = [0, lead] + list(range(1, lead))
    for i, b in enumerate(order):
        step(b)
        if i == 0:
            pl.semaphore_wait(barrier, n_rows + n_model - 2)
        for k in range(1, n_rows):
            sum_copy(b, k).start()
    for k in range(1, n_model):
        gain_model(k).start()

    for b in order:
        a, start, width = blocks[b]
        for k in range(1, n_rows):
            wait_sum(b, k)
        total = sums[b, 0]
        for k in range(1, n_rows):
            total = total + sums[b, k]
        column = total / d_model
        cols[a][:, pl.ds(start, width)] = column
        scale = jnp.broadcast_to(1.0 / column, (TILE, width))

        def one(i, carry):
            rows = pl.ds(pl.multiple_of(i * TILE, TILE), TILE)
            there = pl.ds(pl.multiple_of(me * share + i * TILE, TILE), TILE)
            where = pl.ds(start, width)
            finals[a][there, where] = (results[a][rows, where] * scale).astype(jnp.bfloat16)
            return carry

        lax.fori_loop(0, share // TILE, one, 0)
        if b != lead:
            both_ways(z, b)
        to_side(z, b).start()
    both_ways(z, lead)

    for k in range(1, n_model):
        who = lax.rem(col + n_model - k, n_model)
        pltpu.make_async_remote_copy(
            src_ref=gains.at[me, who],
            dst_ref=gains.at[me, who],
            send_sem=gain_send.at[k],
            recv_sem=gain_recv.at[k],
            device_id={"model": lax.rem(col + k, n_model)},
            device_id_type=MESH,
        ).wait_recv()
    for k in range(1, n_rows):
        gain_rows(k, me).start()

    to_side(z, lead, False).wait_recv()
    both_ways(z, nb)

    for d in range(1, line):
        for j in range(nb + 1):

            @pl.when(z - d >= 0)
            def _():
                to_line(z - d, j, True).wait_recv()

                @pl.when(z < line - 1)
                def _():
                    to_line(z - d, j, True).start()

                if j < lead:
                    to_side(z - d, j).start()

            @pl.when(z + d < line)
            def _():
                to_line(z + d, j, False).wait_recv()

                @pl.when(z > 0)
                def _():
                    to_line(z + d, j, False).start()

                if j < lead:
                    to_side(z + d, j).start()

    for k in range(1, n_rows):
        gain_rows(k, lax.rem(me + n_rows - k, n_rows)).wait_recv()
    for r in range(n_rows):
        for m in range(n_model):
            norm_out[pl.ds(r * n_model + m, 1), :] = gains[r, m]

    for zs in range(line):
        for j in range(lead):
            to_side(zs, j, False).wait_recv()
    for k in range(1, n_model):
        gain_model(k).wait_send()
    for k in range(1, n_rows):
        gain_rows(k, me).wait_send()
        for b in range(nb):
            sum_copy(b, k).wait_send()
    for zs in range(line):
        for j in range(lead):
            to_side(zs, j).wait_send()
        for j in range(nb + 1):

            @pl.when((z > 0) & (z <= zs))
            def _():
                to_line(zs, j, False).wait_send()

            @pl.when((z < line - 1) & (z >= zs))
            def _():
                to_line(zs, j, True).wait_send()
    to_side(z, lead).wait_send()


def write(pieces, *refs):
    ins, outs, sem = refs[:10], refs[10:20], refs[20]
    copies = []
    for n, (i, start, rows) in enumerate(pieces):
        where = pl.ds(start, rows)
        c = pltpu.make_async_copy(ins[i].at[where], outs[i].at[where], sem.at[n])
        c.start()
        copies.append(c)
    outs[6][...] = ins[6][...].astype(jnp.bfloat16)
    for c in copies:
        c.wait()


def fused(n_rows, n_model, d_model, blocks, arrays):
    *weights, norm_train, norm_step = arrays
    share = weights[0].shape[0]
    widths = [weights[3 * a].shape[1] for a in range(3)]
    line, nb = n_rows // SIDE, len(blocks)
    unit = norm_train.shape[0]
    anywhere = pl.BlockSpec(memory_space=pl.ANY)
    vmem = pl.BlockSpec(memory_space=pltpu.VMEM)
    f32, dma = jnp.float32, pltpu.SemaphoreType.DMA
    out = pl.pallas_call(
        functools.partial(kernel, n_rows, n_model, blocks, d_model),
        out_shape=[
            *(pltpu.VMEM((d_model, w), jnp.bfloat16) for w in widths),
            *(pltpu.VMEM((1, w), f32) for w in widths),
            pltpu.VMEM((n_rows * n_model, unit), f32),
            *(pltpu.VMEM((share, w), f32) for w in widths),
        ],
        in_specs=[anywhere] * 9 + [vmem] * 2,
        out_specs=[vmem] * 10,
        scratch_shapes=[
            *(pltpu.VMEM((share, w), f32) for w in widths for _ in range(3)),
            pltpu.VMEM((nb, n_rows, 1, blocks[0][2]), f32),
            pltpu.VMEM((n_rows, n_model, 1, unit), f32),
            dma((nb, 3)),
            dma((nb, n_rows)),
            dma((nb, n_rows)),
            dma((n_rows + n_model,)),
            dma((n_rows + n_model,)),
            dma((line, nb + 1)),
            dma((line, nb + 1)),
            dma((line, nb)),
            dma((line, nb + 1)),
            dma((line, nb)),
        ],
        compiler_params=pltpu.CompilerParams(
            collective_id=0, has_side_effects=True, vmem_limit_bytes=48 * 2**20
        ),
    )(*weights, norm_train.reshape(1, -1), norm_step.reshape(1, -1))
    pieces = []
    for i in [0, 7, 1, 2, 8, 9, 3, 4, 5]:
        rows = out[i].shape[0]
        cut = rows // PIECES if i == 0 else rows
        pieces += [(i, r, cut) for r in range(0, rows, cut)]
    done = pl.pallas_call(
        functools.partial(write, pieces),
        out_shape=[
            jax.ShapeDtypeStruct(o.shape, jnp.bfloat16 if i == 6 else o.dtype)
            for i, o in enumerate(out)
        ],
        in_specs=[vmem if i == 6 else anywhere for i in range(10)],
        out_specs=[vmem if i == 6 else anywhere for i in range(10)],
        scratch_shapes=[dma((len(pieces),))],
        compiler_params=pltpu.CompilerParams(vmem_limit_bytes=2**20),
    )(*out)
    return tuple(d.reshape(-1) if 3 <= i <= 6 else d for i, d in enumerate(done))


def solution(mesh):
    n_rows, n_model = mesh.shape["rows"], mesh.shape["model"]

    def body(*arrays):
        share = arrays[0].shape[0]
        widths = [arrays[3 * a].shape[1] for a in range(3)]
        width = min(widths)
        d_model = share * n_rows
        fits = (
            n_rows % SIDE == 0
            and 2 <= n_rows // SIDE <= 4
            and share % TILE == 0
            and width % 128 == 0
            and all(w % width == 0 for w in widths)
        )
        if not fits:
            return plain(d_model, arrays)
        blocks = tuple(
            (a, s, width) for a, w in enumerate(widths) for s in range(0, w, width)
        )
        return fused(n_rows, n_model, d_model, blocks, arrays)

    return jax.shard_map(
        body,
        mesh=mesh,
        in_specs=(P("rows", "model"),) * 9 + (P(("rows", "model")),) * 2,
        out_specs=(
            *(P(None, "model"),) * 3,
            *(P("model"),) * 3,
            P(),
            *(P("rows", "model"),) * 3,
        ),
        check_vma=False,
    )
```

profile of v0, /device:TPU:0, one launch (start us, length us, event | category | flops | bytes accessed | tf_op | source)
XLA Modules:
  0.0 138.8 jit_solution(5352346169991653270)
XLA Ops:
  0.6 131.9 %shard_map.186 = (bf16[4096,1024]{1,0:T(8,128)(2,1)S(1)}, bf16[4096,256]{1,0:T(8,128)(2,1)S(1)}, bf16[4096,256]{1,0:T(8,128)(2,1)S(1)}, f32[1,1024]{1,0:T(1,128)...) custom-call(f32[512,1024]{1,0:T(8,128)} %refs_0_.1, ...), custom_call_target="tpu_custom_call" | custom-call | tf_op jit(solution)/shard_map/pallas_call | solution.py:301
  132.6 6.2 %shard_map.187 = (bf16[4096,1024]{1,0:T(8,128)(2,1)}, bf16[4096,256]{1,0:T(8,128)(2,1)}, bf16[4096,256]{1,0:T(8,128)(2,1)}, f32[1,1024]{1,0:T(1,128)}, f32[1,256...) custom-call(bf16[4096,1024]{1,0:T(8,128)(2,1)S(1)} %get-tuple-elemen, ...), custom_call_target="tpu_custom_call" | custom-call | tf_op jit(solution)/shard_map/pallas_call | solution.py:335
where the time goes:
time: 139 us
  Pallas kernels  138 us (99%)
    pallas_call x1, Pallas kernels, fused(): pl.pallas_call(functools.partial(kernel, n_rows, n_model, blocks, d_model...  132 us
    pallas_call x1, Pallas kernels, fused(): pl.pallas_call(functools.partial(write, pieces), out_shape=[jax.ShapeDtyp...  6.2 us

commit v1 on v0

--- a/solution.py
+++ b/solution.py
@@ -43,28 +43,18 @@
     ins, refs = refs[:9], refs[9:]
     nt_ref, ns_ref = refs[:2]
     finals, cols, norm_out, results = refs[2:5], refs[5:8], refs[8], refs[9:12]
-    bufs = refs[12:21]
-    (sums, gains, in_sem, sum_send, sum_recv, gain_send, gain_recv,
-     up_send, down_send, side_send, line_recv, side_recv) = refs[21:]
+    bufs = refs[12:15]
+    (norms, sums, gains, in_sem, norm_sem, sum_send, sum_recv, gain_send, gain_recv,
+     up_send, down_send, side_send, line_recv, side_recv) = refs[15:]
 
     line = n_rows // SIDE
     me = lax.axis_index("rows")
     col = lax.axis_index("model")
     z, y = me // SIDE, me % SIDE
     other = 1 - y
-    share = bufs[0].shape[0]
+    share = bufs[0].shape[1]
     nb = len(blocks)
     lead = nb - 1
-
-    loads = []
-    for b, (a, start, width) in enumerate(blocks):
-        for k in range(3):
-            where = (slice(None), pl.ds(start, width))
-            c = pltpu.make_async_copy(
-                ins[3 * a + k].at[where], bufs[3 * a + k].at[where], in_sem.at[b, k]
-            )
-            c.start()
-            loads.append(c)
 
     barrier = pltpu.get_barrier_semaphore()
     for k in range(1, n_rows):
@@ -75,17 +65,31 @@
         pl.semaphore_signal(
             barrier, inc=1, device_id={"model": lax.rem(col + k, n_model)}, device_id_type=MESH
         )
-    gains[me, col] = nt_ref[...] + ns_ref[...]
+
+    def load(b):
+        a, start, width = blocks[b]
+        where = (slice(None), pl.ds(start, width))
+        for k in range(3):
+            pltpu.make_async_copy(
+                ins[3 * a + k].at[where], bufs[a].at[(k, *where)], in_sem.at[b]
+            ).start()
+
+    def wait_bytes(ref, sem):
+        pltpu.make_async_copy(ref, ref, sem).wait()
 
     def step(b):
         a, start, width = blocks[b]
-        for k in range(3):
-            loads[3 * b + k].wait()
+        wait_bytes(bufs[a].at[:, :, pl.ds(start, width)], in_sem.at[b])
+        if b == 0:
+            for other_b in order[1:]:
+                load(other_b)
+            for n, ref in enumerate((nt_ref, ns_ref)):
+                pltpu.make_async_copy(ref, norms.at[n], norm_sem.at[0]).start()
 
         def one(i, acc):
             rows = pl.ds(pl.multiple_of(i * TILE, TILE), TILE)
             where = (rows, pl.ds(start, width))
-            r = adam(*(bufs[3 * a + k][where] for k in range(3)))
+            r = adam(*(bufs[a][(k, *where)] for k in range(3)))
             results[a][where] = r
             m = jnp.abs(r).reshape(TILE // 8, 8, width)
             return acc + jnp.sum(m, axis=0)
@@ -97,36 +101,30 @@
         return pltpu.make_async_remote_copy(
             src_ref=sums.at[b, me],
             dst_ref=sums.at[b, me],
-            send_sem=sum_send.at[b, k],
-            recv_sem=sum_recv.at[b, k],
+            send_sem=sum_send.at[0],
+            recv_sem=sum_recv.at[b],
             device_id={"rows": lax.rem(me + k, n_rows)},
             device_id_type=MESH,
         )
-
-    def wait_sum(b, k):
-        who = lax.rem(me + n_rows - k, n_rows)
-        pltpu.make_async_remote_copy(
-            src_ref=sums.at[b, who],
-            dst_ref=sums.at[b, who],
-            send_sem=sum_send.at[b, k],
-            recv_sem=sum_recv.at[b, k],
-            device_id={"rows": lax.rem(me + k, n_rows)},
-            device_id_type=MESH,
-        ).wait_recv()
 
     def place(j, owner):
         a, start, width = blocks[j]
         rows = pl.ds(pl.multiple_of(owner * share, share), share)
         return finals[a].at[rows, pl.ds(start, width)]
 
-    def to_line(zs, j, up):
+    def some(n):
+        w = finals[0].shape[1]
+        return finals[0].at[pl.ds(0, n * share * blocks[0][2] // w)]
+
+    def to_line(zs, j, up, to):
         owner = zs * SIDE + (other if j == nb else y)
         part = place(min(j, lead), owner)
+        slot = jnp.where(zs < to, zs, zs - 1)
         return pltpu.make_async_remote_copy(
             src_ref=part,
             dst_ref=part,
-            send_sem=(up_send if up else down_send).at[zs, j],
-            recv_sem=line_recv.at[zs, j],
+            send_sem=(up_send if up else down_send).at[zs],
+            recv_sem=line_recv.at[slot, j],
             device_id={"rows": me + (SIDE if up else -SIDE)},
             device_id_type=MESH,
         )
@@ -136,8 +134,8 @@
         return pltpu.make_async_remote_copy(
             src_ref=part,
             dst_ref=part,
-            send_sem=side_send.at[zs, j],
-            recv_sem=side_recv.at[zs, j],
+            send_sem=side_send.at[0],
+            recv_sem=side_recv.at[1 if j == lead else 0],
             device_id={"rows": z * SIDE + other},
             device_id_type=MESH,
         )
@@ -145,46 +143,48 @@
     def both_ways(zs, j):
         @pl.when(z > 0)
         def _():
-            to_line(zs, j, False).start()
+            to_line(zs, j, False, z - 1).start()
 
         @pl.when(z < line - 1)
         def _():
-            to_line(zs, j, True).start()
+            to_line(zs, j, True, z + 1).start()
 
     def gain_model(k):
         return pltpu.make_async_remote_copy(
             src_ref=gains.at[me, col],
             dst_ref=gains.at[me, col],
-            send_sem=gain_send.at[k],
-            recv_sem=gain_recv.at[k],
+            send_sem=gain_send.at[0],
+            recv_sem=gain_recv.at[0],
             device_id={"model": lax.rem(col + k, n_model)},
             device_id_type=MESH,
         )
 
-    def gain_rows(k, who):
-        return pltpu.make_async_remote_copy(
-            src_ref=gains.at[who],
-            dst_ref=gains.at[who],
-            send_sem=gain_send.at[n_model + k],
-            recv_sem=gain_recv.at[n_model + k],
+    def gain_rows(k):
+        return pltpu.make_async_remote_copy(
+            src_ref=gains.at[me],
+            dst_ref=gains.at[me],
+            send_sem=gain_send.at[1],
+            recv_sem=gain_recv.at[1],
             device_id={"rows": lax.rem(me + k, n_rows)},
             device_id_type=MESH,
         )
 
     order = [0, lead] + list(range(1, lead))
+    load(0)
     for i, b in enumerate(order):
         step(b)
         if i == 0:
             pl.semaphore_wait(barrier, n_rows + n_model - 2)
         for k in range(1, n_rows):
             sum_copy(b, k).start()
+    wait_bytes(norms, norm_sem.at[0])
+    gains[me, col] = norms[0] + norms[1]
     for k in range(1, n_model):
         gain_model(k).start()
 
     for b in order:
         a, start, width = blocks[b]
-        for k in range(1, n_rows):
-            wait_sum(b, k)
+        wait_bytes(sums.at[b, pl.ds(0, n_rows - 1)], sum_recv.at[b])
         total = sums[b, 0]
         for k in range(1, n_rows):
             total = total + sums[b, k]
@@ -205,75 +205,58 @@
         to_side(z, b).start()
     both_ways(z, lead)
 
-    for k in range(1, n_model):
-        who = lax.rem(col + n_model - k, n_model)
-        pltpu.make_async_remote_copy(
-            src_ref=gains.at[me, who],
-            dst_ref=gains.at[me, who],
-            send_sem=gain_send.at[k],
-            recv_sem=gain_recv.at[k],
-            device_id={"model": lax.rem(col + k, n_model)},
-            device_id_type=MESH,
-        ).wait_recv()
+    wait_bytes(gains.at[0, pl.ds(0, n_model - 1)], gain_recv.at[0])
     for k in range(1, n_rows):
-        gain_rows(k, me).start()
+        gain_rows(k).start()
 
     to_side(z, lead, False).wait_recv()
     both_ways(z, nb)
 
-    for d in range(1, line):
-        for j in range(nb + 1):
-
-            @pl.when(z - d >= 0)
-            def _():
-                to_line(z - d, j, True).wait_recv()
-
-                @pl.when(z < line - 1)
-                def _():
-                    to_line(z - d, j, True).start()
-
-                if j < lead:
-                    to_side(z - d, j).start()
-
-            @pl.when(z + d < line)
-            def _():
-                to_line(z + d, j, False).wait_recv()
-
-                @pl.when(z > 0)
-                def _():
-                    to_line(z + d, j, False).start()
-
-                if j < lead:
-                    to_side(z + d, j).start()
-
-    for k in range(1, n_rows):
-        gain_rows(k, lax.rem(me + n_rows - k, n_rows)).wait_recv()
+    wait_bytes(gains.at[pl.ds(0, n_rows - 1)], gain_recv.at[1])
     for r in range(n_rows):
         for m in range(n_model):
             norm_out[pl.ds(r * n_model + m, 1), :] = gains[r, m]
 
+    for d in range(1, line):
+        for j in range(nb + 1):
+
+            @pl.when(z - d >= 0)
+            def _():
+                to_line(z - d, j, True, z).wait_recv()
+
+                @pl.when(z < line - 1)
+                def _():
+                    to_line(z - d, j, True, z + 1).start()
+
+                if j < lead:
+                    to_side(z - d, j).start()
+
+            @pl.when(z + d < line)
+            def _():
+                to_line(z + d, j, False, z).wait_recv()
+
+                @pl.when(z > 0)
+                def _():
+                    to_line(z + d, j, False, z - 1).start()
+
+                if j < lead:
+                    to_side(z + d, j).start()
+
+    wait_bytes(gains.at[0, pl.ds(0, n_model - 1)], gain_send.at[0])
+    wait_bytes(gains.at[pl.ds(0, n_rows - 1)], gain_send.at[1])
+    wait_bytes(sums.at[:, pl.ds(0, n_rows - 1)], sum_send.at[0])
     for zs in range(line):
-        for j in range(lead):
-            to_side(zs, j, False).wait_recv()
-    for k in range(1, n_model):
-        gain_model(k).wait_send()
-    for k in range(1, n_rows):
-        gain_rows(k, me).wait_send()
-        for b in range(nb):
-            sum_copy(b, k).wait_send()
-    for zs in range(line):
-        for j in range(lead):
-            to_side(zs, j).wait_send()
-        for j in range(nb + 1):
-
-            @pl.when((z > 0) & (z <= zs))
-            def _():
-                to_line(zs, j, False).wait_send()
-
-            @pl.when((z < line - 1) & (z >= zs))
-            def _():
-                to_line(zs, j, True).wait_send()
-    to_side(z, lead).wait_send()
+
+        @pl.when((z > 0) & (z <= zs))
+        def _():
+            wait_bytes(some(nb + 1), down_send.at[zs])
+
+        @pl.when((z < line - 1) & (z >= zs))
+        def _():
+            wait_bytes(some(nb + 1), up_send.at[zs])
+
+    wait_bytes(some(line * lead), side_recv.at[0])
+    wait_bytes(some(line * lead + 1), side_send.at[0])
 
 
 def write(pieces, *refs):
@@ -306,22 +289,24 @@
             pltpu.VMEM((n_rows * n_model, unit), f32),
             *(pltpu.VMEM((share, w), f32) for w in widths),
         ],
-        in_specs=[anywhere] * 9 + [vmem] * 2,
+        in_specs=[anywhere] * 11,
         out_specs=[vmem] * 10,
         scratch_shapes=[
-            *(pltpu.VMEM((share, w), f32) for w in widths for _ in range(3)),
+            *(pltpu.VMEM((3, share, w), f32) for w in widths),
+            pltpu.VMEM((2, 1, unit), f32),
             pltpu.VMEM((nb, n_rows, 1, blocks[0][2]), f32),
             pltpu.VMEM((n_rows, n_model, 1, unit), f32),
-            dma((nb, 3)),
-            dma((nb, n_rows)),
-            dma((nb, n_rows)),
-            dma((n_rows + n_model,)),
-            dma((n_rows + n_model,)),
-            dma((line, nb + 1)),
-            dma((line, nb + 1)),
-            dma((line, nb)),
-            dma((line, nb + 1)),
-            dma((line, nb)),
+            dma((nb,)),
+            dma((1,)),
+            dma((1,)),
+            dma((nb,)),
+            dma((2,)),
+            dma((2,)),
+            dma((line,)),
+            dma((line,)),
+            dma((1,)),
+            dma((line - 1, nb + 1)),
+            dma((2,)),
         ],
         compiler_params=pltpu.CompilerParams(
             collective_id=0, has_side_effects=True, vmem_limit_bytes=48 * 2**20
@@ -360,6 +345,7 @@
             and share % TILE == 0
             and width % 128 == 0
             and all(w % width == 0 for w in widths)
+            and sum(widths) + width <= 2 * widths[0]
         )
         if not fits:
             return plain(d_model, arrays)

time: 139 us -> 137 us (0.986)
  Pallas kernels: 138 us -> 136 us
    pallas_call x1, Pallas kernels: 132 us -> 130 us  [fused(): pl.pallas_call(functools.partial(kernel, n_rows, n_model, blocks, d_model...]
where the time goes in v1:
time: 137 us
  Pallas kernels  136 us (99%)
    pallas_call x1, Pallas kernels, fused(): pl.pallas_call(functools.partial(kernel, n_rows, n_model, blocks, d_model...  130 us
    pallas_call x1, Pallas kernels, fused(): pl.pallas_call(functools.partial(write, pieces), out_shape=[jax.ShapeDtyp...  6.2 us

profile of v1, /device:TPU:0, one launch (start us, length us, event | category | flops | bytes accessed | tf_op | source)
XLA Modules:
  0.0 137.1 jit_solution(8619922277854945202)
XLA Ops:
  0.6 130.2 %shard_map.186 = (bf16[4096,1024]{1,0:T(8,128)(2,1)S(1)}, bf16[4096,256]{1,0:T(8,128)(2,1)S(1)}, bf16[4096,256]{1,0:T(8,128)(2,1)S(1)}, f32[1,1024]{1,0:T(1,128)...) custom-call(f32[512,1024]{1,0:T(8,128)} %refs_0_.1, ...), custom_call_target="tpu_custom_call" | custom-call | tf_op jit(solution)/shard_map/pallas_call | solution.py:284
  130.8 6.2 %shard_map.187 = (bf16[4096,1024]{1,0:T(8,128)(2,1)}, bf16[4096,256]{1,0:T(8,128)(2,1)}, bf16[4096,256]{1,0:T(8,128)(2,1)}, f32[1,1024]{1,0:T(1,128)}, f32[1,256...) custom-call(bf16[4096,1024]{1,0:T(8,128)(2,1)S(1)} %get-tuple-elemen, ...), custom_call_target="tpu_custom_call" | custom-call | tf_op jit(solution)/shard_map/pallas_call | solution.py:320

commit v2 on v1

--- a/solution.py
+++ b/solution.py
@@ -15,6 +15,7 @@
 SIDE = 2
 TILE = 32
 PIECES = 4
+EARLY = 128
 
 
 def adam(w, first, second):
@@ -44,8 +45,8 @@
     nt_ref, ns_ref = refs[:2]
     finals, cols, norm_out, results = refs[2:5], refs[5:8], refs[8], refs[9:12]
     bufs = refs[12:15]
-    (norms, sums, gains, in_sem, norm_sem, sum_send, sum_recv, gain_send, gain_recv,
-     up_send, down_send, side_send, line_recv, side_recv) = refs[15:]
+    (norms, lines, sums, gains, in_sem, norm_sem, sum_send, sum_recv, gain_send, gain_recv,
+     up_send, down_send, side_send, line_recv, side_recv, own_send, early, early_send, early_recv) = refs[15:]
 
     line = n_rows // SIDE
     me = lax.axis_index("rows")
@@ -107,30 +108,41 @@
             device_id_type=MESH,
         )
 
-    def place(j, owner):
+    def place(j, owner, late=False):
         a, start, width = blocks[j]
-        rows = pl.ds(pl.multiple_of(owner * share, share), share)
+        skip = EARLY if late and j == 0 else 0
+        rows = pl.ds(pl.multiple_of(owner * share + skip, 16), share - skip)
         return finals[a].at[rows, pl.ds(start, width)]
 
-    def some(n):
-        w = finals[0].shape[1]
-        return finals[0].at[pl.ds(0, n * share * blocks[0][2] // w)]
-
-    def to_line(zs, j, up, to):
+    def some(n, late=False):
+        rows = n * share - (EARLY if late else 0)
+        return finals[0].at[pl.ds(0, rows * blocks[0][2] // finals[0].shape[1])]
+
+    def early_copy(n, to):
+        return pltpu.make_async_remote_copy(
+            src_ref=results[0].at[pl.ds(0, EARLY), pl.ds(0, blocks[0][2])],
+            dst_ref=early.at[n],
+            send_sem=early_send.at[n],
+            recv_sem=early_recv.at[n],
+            device_id={"rows": to},
+            device_id_type=MESH,
+        )
+
+    def to_line(zs, j, up, to, late=False, own=False):
         owner = zs * SIDE + (other if j == nb else y)
-        part = place(min(j, lead), owner)
+        part = place(min(j, lead), owner, late)
         slot = jnp.where(zs < to, zs, zs - 1)
         return pltpu.make_async_remote_copy(
             src_ref=part,
             dst_ref=part,
-            send_sem=(up_send if up else down_send).at[zs],
+            send_sem=own_send.at[int(up)] if own else (up_send if up else down_send).at[zs],
             recv_sem=line_recv.at[slot, j],
             device_id={"rows": me + (SIDE if up else -SIDE)},
             device_id_type=MESH,
         )
 
-    def to_side(zs, j, mine=True):
-        part = place(j, zs * SIDE + (y if mine else other))
+    def to_side(zs, j, mine=True, late=False):
+        part = place(j, zs * SIDE + (y if mine else other), late)
         return pltpu.make_async_remote_copy(
             src_ref=part,
             dst_ref=part,
@@ -140,14 +152,14 @@
             device_id_type=MESH,
         )
 
-    def both_ways(zs, j):
+    def both_ways(j):
         @pl.when(z > 0)
         def _():
-            to_line(zs, j, False, z - 1).start()
+            to_line(z, j, False, z - 1, True, True).start()
 
         @pl.when(z < line - 1)
         def _():
-            to_line(zs, j, True, z + 1).start()
+            to_line(z, j, True, z + 1, True, True).start()
 
     def gain_model(k):
         return pltpu.make_async_remote_copy(
@@ -177,6 +189,16 @@
             pl.semaphore_wait(barrier, n_rows + n_model - 2)
         for k in range(1, n_rows):
             sum_copy(b, k).start()
+        if i == 0:
+            early_copy(0, z * SIDE + other).start()
+
+            @pl.when(z < line - 1)
+            def _():
+                early_copy(1, me + SIDE).start()
+
+            @pl.when(z > 0)
+            def _():
+                early_copy(2, me - SIDE).start()
     wait_bytes(norms, norm_sem.at[0])
     gains[me, col] = norms[0] + norms[1]
     for k in range(1, n_model):
@@ -201,28 +223,53 @@
 
         lax.fori_loop(0, share // TILE, one, 0)
         if b != lead:
-            both_ways(z, b)
-        to_side(z, b).start()
-    both_ways(z, lead)
+            both_ways(b)
+        to_side(z, b, late=True).start()
+    both_ways(lead)
+
+    width = blocks[0][2]
+    scale = jnp.broadcast_to(1.0 / cols[0][:, pl.ds(0, width)], (TILE, width))
+
+    def finish(n, owner):
+        early_copy(n, owner).wait_recv()
+
+        def one(i, carry):
+            rows = pl.ds(pl.multiple_of(i * TILE, TILE), TILE)
+            there = pl.ds(pl.multiple_of(owner * share + i * TILE, TILE), TILE)
+            finals[0][there, pl.ds(0, width)] = (early[n, rows] * scale).astype(jnp.bfloat16)
+            return carry
+
+        lax.fori_loop(0, EARLY // TILE, one, 0)
+
+    @pl.when(z > 0)
+    def _():
+        finish(1, me - SIDE)
+
+    @pl.when(z < line - 1)
+    def _():
+        finish(2, me + SIDE)
+
+    finish(0, z * SIDE + other)
 
     wait_bytes(gains.at[0, pl.ds(0, n_model - 1)], gain_recv.at[0])
     for k in range(1, n_rows):
         gain_rows(k).start()
 
     to_side(z, lead, False).wait_recv()
-    both_ways(z, nb)
+    both_ways(nb)
 
     wait_bytes(gains.at[pl.ds(0, n_rows - 1)], gain_recv.at[1])
     for r in range(n_rows):
         for m in range(n_model):
-            norm_out[pl.ds(r * n_model + m, 1), :] = gains[r, m]
+            lines[pl.ds(r * n_model + m, 1), :] = gains[r, m]
+    norm_out[...] = lines[...].astype(jnp.bfloat16)
 
     for d in range(1, line):
         for j in range(nb + 1):
 
             @pl.when(z - d >= 0)
             def _():
-                to_line(z - d, j, True, z).wait_recv()
+                to_line(z - d, j, True, z, d == 1).wait_recv()
 
                 @pl.when(z < line - 1)
                 def _():
@@ -233,7 +280,7 @@
 
             @pl.when(z + d < line)
             def _():
-                to_line(z + d, j, False, z).wait_recv()
+                to_line(z + d, j, False, z, d == 1).wait_recv()
 
                 @pl.when(z > 0)
                 def _():
@@ -245,18 +292,30 @@
     wait_bytes(gains.at[0, pl.ds(0, n_model - 1)], gain_send.at[0])
     wait_bytes(gains.at[pl.ds(0, n_rows - 1)], gain_send.at[1])
     wait_bytes(sums.at[:, pl.ds(0, n_rows - 1)], sum_send.at[0])
+    early_copy(0, me).wait_send()
+
+    @pl.when(z < line - 1)
+    def _():
+        early_copy(1, me).wait_send()
+        wait_bytes(some(nb + 1, True), own_send.at[1])
+
+    @pl.when(z > 0)
+    def _():
+        early_copy(2, me).wait_send()
+        wait_bytes(some(nb + 1, True), own_send.at[0])
+
     for zs in range(line):
 
-        @pl.when((z > 0) & (z <= zs))
+        @pl.when((z > 0) & (z < zs))
         def _():
             wait_bytes(some(nb + 1), down_send.at[zs])
 
-        @pl.when((z < line - 1) & (z >= zs))
+        @pl.when((z < line - 1) & (z > zs))
         def _():
             wait_bytes(some(nb + 1), up_send.at[zs])
 
-    wait_bytes(some(line * lead), side_recv.at[0])
-    wait_bytes(some(line * lead + 1), side_send.at[0])
+    wait_bytes(some(line * lead, True), side_recv.at[0])
+    wait_bytes(some(line * lead + 1, True), side_send.at[0])
 
 
 def write(pieces, *refs):
@@ -267,7 +326,6 @@
         c = pltpu.make_async_copy(ins[i].at[where], outs[i].at[where], sem.at[n])
         c.start()
         copies.append(c)
-    outs[6][...] = ins[6][...].astype(jnp.bfloat16)
     for c in copies:
         c.wait()
 
@@ -286,7 +344,7 @@
         out_shape=[
             *(pltpu.VMEM((d_model, w), jnp.bfloat16) for w in widths),
             *(pltpu.VMEM((1, w), f32) for w in widths),
-            pltpu.VMEM((n_rows * n_model, unit), f32),
+            pltpu.VMEM((n_rows * n_model, unit), jnp.bfloat16),
             *(pltpu.VMEM((share, w), f32) for w in widths),
         ],
         in_specs=[anywhere] * 11,
@@ -294,6 +352,7 @@
         scratch_shapes=[
             *(pltpu.VMEM((3, share, w), f32) for w in widths),
             pltpu.VMEM((2, 1, unit), f32),
+            pltpu.VMEM((n_rows * n_model, unit), f32),
             pltpu.VMEM((nb, n_rows, 1, blocks[0][2]), f32),
             pltpu.VMEM((n_rows, n_model, 1, unit), f32),
             dma((nb,)),
@@ -307,24 +366,25 @@
             dma((1,)),
             dma((line - 1, nb + 1)),
             dma((2,)),
+            dma((2,)),
+            pltpu.VMEM((3, EARLY, blocks[0][2]), f32),
+            dma((3,)),
+            dma((3,)),
         ],
         compiler_params=pltpu.CompilerParams(
             collective_id=0, has_side_effects=True, vmem_limit_bytes=48 * 2**20
         ),
     )(*weights, norm_train.reshape(1, -1), norm_step.reshape(1, -1))
     pieces = []
-    for i in [0, 7, 1, 2, 8, 9, 3, 4, 5]:
+    for i in [0, 7, 1, 2, 8, 9, 3, 4, 5, 6]:
         rows = out[i].shape[0]
         cut = rows // PIECES if i == 0 else rows
         pieces += [(i, r, cut) for r in range(0, rows, cut)]
     done = pl.pallas_call(
         functools.partial(write, pieces),
-        out_shape=[
-            jax.ShapeDtypeStruct(o.shape, jnp.bfloat16 if i == 6 else o.dtype)
-            for i, o in enumerate(out)
-        ],
-        in_specs=[vmem if i == 6 else anywhere for i in range(10)],
-        out_specs=[vmem if i == 6 else anywhere for i in range(10)],
+        out_shape=[jax.ShapeDtypeStruct(o.shape, o.dtype) for o in out],
+        in_specs=[anywhere] * 10,
+        out_specs=[anywhere] * 10,
         scratch_shapes=[dma((len(pieces),))],
         compiler_params=pltpu.CompilerParams(vmem_limit_bytes=2**20),
     )(*out)
@@ -343,6 +403,7 @@
             n_rows % SIDE == 0
             and 2 <= n_rows // SIDE <= 4
             and share % TILE == 0
+            and share > EARLY
             and width % 128 == 0
             and all(w % width == 0 for w in widths)
             and sum(widths) + width <= 2 * widths[0]

time: 137 us -> 135 us (0.985)
  no operation moved by 1% of the time
where the time goes in v2:
time: 135 us
  Pallas kernels  135 us (100%)
    pallas_call x1, Pallas kernels, fused(): pl.pallas_call(functools.partial(kernel, n_rows, n_model, blocks, d_model...  129 us
    pallas_call x1, Pallas kernels, fused(): pl.pallas_call(functools.partial(write, pieces), out_shape=[jax.ShapeDtyp...  5.62 us

profile of v2, /device:TPU:0, one launch (start us, length us, event | category | flops | bytes accessed | tf_op | source)
XLA Modules:
  0.0 135.3 jit_solution(1588578498160698843)
XLA Ops:
  0.6 129.1 %shard_map.186 = (bf16[4096,1024]{1,0:T(8,128)(2,1)S(1)}, bf16[4096,256]{1,0:T(8,128)(2,1)S(1)}, bf16[4096,256]{1,0:T(8,128)(2,1)S(1)}, f32[1,1024]{1,0:T(1,128)...) custom-call(f32[512,1024]{1,0:T(8,128)} %refs_0_.1, ...), custom_call_target="tpu_custom_call" | custom-call | tf_op jit(solution)/shard_map/pallas_call | solution.py:342
  129.7 5.6 %shard_map.187 = (bf16[4096,1024]{1,0:T(8,128)(2,1)}, bf16[4096,256]{1,0:T(8,128)(2,1)}, bf16[4096,256]{1,0:T(8,128)(2,1)}, f32[1,1024]{1,0:T(1,128)}, f32[1,256...) custom-call(bf16[4096,1024]{1,0:T(8,128)(2,1)S(1)} %get-tuple-elemen, ...), custom_call_target="tpu_custom_call" | custom-call | tf_op jit(solution)/shard_map/pallas_call | solution.py:383

commit v3 on v1

v3 whole, which is shorter than its diff:
```python
import functools

import jax
import jax.numpy as jnp
from jax import lax
from jax.experimental import pallas as pl
from jax.experimental.pallas import tpu as pltpu
from jax.sharding import PartitionSpec as P

learn_rate = 0.01
decay_rate = 0.05
tiny_value = 1e-08

MESH = pl.DeviceIdType.MESH
SIDE = 2
TILE = 32
EARLY = 128
PAIR = 1


def adam(w, first, second):
    return w - learn_rate * (first / (jnp.sqrt(second) + tiny_value) + decay_rate * w)


def plain(d_model, arrays):
    *weights, norm_train, norm_step = arrays
    results = [adam(*weights[3 * i : 3 * i + 3]) for i in range(3)]
    totals = lax.psum(tuple(jnp.sum(jnp.abs(r), axis=0) for r in results), "rows")
    columns = [t / d_model for t in totals]
    finals = [
        lax.all_gather((r / c).astype(jnp.bfloat16), "rows", axis=0, tiled=True)
        for r, c in zip(results, columns)
    ]
    serve = lax.all_gather(
        (norm_train + norm_step).astype(jnp.bfloat16), ("rows", "model"), axis=0, tiled=True
    )
    return (*finals, *columns, serve, *results)


def wait_bytes(ref, sem):
    pltpu.make_async_copy(ref, ref, sem).wait()


def on_core(work):
    core = lax.axis_index("model") % 2
    for c in range(2):
        pl.when(core == c)(functools.partial(work, c))


class Gather:
    def __init__(self, n_rows, share, width, count, skip, whole, own, sems):
        self.line, self.share, self.width = n_rows // SIDE, share, width
        self.count, self.skip, self.whole, self.own = count, skip, whole, own
        (self.own_send, self.up_send, self.down_send, self.side_send,
         self.line_recv, self.side_recv) = sems
        self.me = lax.axis_index("rows")
        self.z, self.y = self.me // SIDE, self.me % SIDE
        self.cut = cut_of(self.line, share, count)
        cut = self.cut
        self.chunks = [(j, 0, share, False) for j in range(count) if j != PAIR]
        self.chunks += [(PAIR, cut, share, False), (PAIR, 0, cut, False), (PAIR, 0, cut, True)]
        self.spread = len(self.chunks) - 2

    def part(self, slot, owner, first, last, ref=None):
        cols = pl.ds(slot * self.width, self.width)
        if ref is not None:
            return ref.at[pl.ds(first, last - first), cols]
        rows = pl.ds(pl.multiple_of(owner * self.share + first, 16), last - first)
        return self.whole.at[rows, cols]

    def some(self, rows):
        return self.whole.at[pl.ds(0, rows // 2), pl.ds(0, 2 * self.width)]

    def to_line(self, zs, c, up, to, near=False, mine=False):
        slot, first, last, crossed = self.chunks[c]
        if near and slot == 0:
            first = self.skip
        owner = zs * SIDE + (1 - self.y if crossed else self.y)
        there = self.part(slot, owner, first, last)
        here = there
        if mine and not crossed:
            here = self.part(slot, owner, first, last, self.own)
        send = self.own_send.at[int(up)] if mine else (self.up_send if up else self.down_send).at[zs]
        return pltpu.make_async_remote_copy(
            src_ref=here,
            dst_ref=there,
            send_sem=send,
            recv_sem=self.line_recv.at[jnp.where(zs < to, zs, zs - 1), c],
            device_id={"rows": self.me + (SIDE if up else -SIDE)},
            device_id_type=MESH,
        )

    def to_side(self, zs, slot, first, from_me=True, mine=False):
        owner = zs * SIDE + (self.y if from_me else 1 - self.y)
        there = self.part(slot, owner, first, self.share)
        here = self.part(slot, owner, first, self.share, self.own) if mine else there
        group = self.line if mine and slot == PAIR else zs
        return pltpu.make_async_remote_copy(
            src_ref=here,
            dst_ref=there,
            send_sem=self.side_send.at[group],
            recv_sem=self.side_recv.at[group],
            device_id={"rows": self.z * SIDE + 1 - self.y},
            device_id_type=MESH,
        )

    def both_ways(self, c):
        z = self.z

        @pl.when(z > 0)
        def _():
            self.to_line(z, c, False, z - 1, True, True).start()

        @pl.when(z < self.line - 1)
        def _():
            self.to_line(z, c, True, z + 1, True, True).start()

    def send_own(self, slot):
        for c, chunk in enumerate(self.chunks):
            if chunk[0] == slot and not chunk[3]:
                self.both_ways(c)
        self.to_side(self.z, slot, self.skip if slot == 0 else 0, mine=True).start()

    def relay(self):
        z, line = self.z, self.line
        self.to_side(z, PAIR, 0, False, True).wait_recv()
        self.both_ways(len(self.chunks) - 1)
        for d in range(1, line):
            for c, (slot, first, _, _) in enumerate(self.chunks):

                @pl.when(z - d >= 0)
                def _():
                    self.to_line(z - d, c, True, z, d == 1).wait_recv()

                    @pl.when(z < line - 1)
                    def _():
                        self.to_line(z - d, c, True, z + 1).start()

                    if c < self.spread:
                        self.to_side(z - d, slot, first).start()

                @pl.when(z + d < line)
                def _():
                    self.to_line(z + d, c, False, z, d == 1).wait_recv()

                    @pl.when(z > 0)
                    def _():
                        self.to_line(z + d, c, False, z - 1).start()

                    if c < self.spread:
                        self.to_side(z + d, slot, first).start()

    def finish(self):
        z, line, share, count, cut = self.z, self.line, self.share, self.count, self.cut
        full = count * share + cut

        @pl.when(z > 0)
        def _():
            wait_bytes(self.some(full - self.skip), self.own_send.at[0])

        @pl.when(z < line - 1)
        def _():
            wait_bytes(self.some(full - self.skip), self.own_send.at[1])

        self.to_side(z, PAIR, 0, mine=True).wait_send()
        for zs in range(line):

            @pl.when((z > 0) & (z < zs))
            def _():
                wait_bytes(self.some(full), self.down_send.at[zs])

            @pl.when((z < line - 1) & (z > zs))
            def _():
                wait_bytes(self.some(full), self.up_send.at[zs])

            for sem in (self.side_recv, self.side_send):

                @pl.when(z == zs)
                def _():
                    wait_bytes(self.some((count - 1) * share - self.skip), sem.at[zs])

                @pl.when(z != zs)
                def _():
                    wait_bytes(self.some(count * share - cut), sem.at[zs])


def cut_of(line, share, count):
    return max(32, round(count * share / (2 * (line - 1)) / 32) * 32)


def gather_sems(line, most):
    dma = pltpu.SemaphoreType.DMA
    return [dma((2,)), dma((line,)), dma((line,)), dma((line + 1,)),
            dma((line - 1, most + 2)), dma((line + 1,))]


def opening(n_rows, n_model, blocks, orders, d_model, *refs):
    ins, refs = refs[:9], refs[9:]
    nt_ref, ns_ref = refs[:2]
    whole, later, cols, norm_out, results = refs[2], refs[3], refs[4:7], refs[7], refs[8:11]
    bufs = refs[11:14]
    (norms, lines, sums, gains, in_sem, norm_sem, sum_send, sum_recv, gain_send, gain_recv,
     early, early_send, early_recv) = refs[14:27]
    sems = refs[27:]

    line = n_rows // SIDE
    me = lax.axis_index("rows")
    col = lax.axis_index("model")
    z, y = me // SIDE, me % SIDE
    other = 1 - y
    share = bufs[0].shape[1]
    width = blocks[0][2]

    def load(b):
        a, start, _ = blocks[b]
        where = (slice(None), pl.ds(start, width))
        for k in range(3):
            pltpu.make_async_copy(
                ins[3 * a + k].at[where], bufs[a].at[(k, *where)], in_sem.at[b]
            ).start()

    on_core(lambda c: load(orders[c][0][0]))
    barrier = pltpu.get_barrier_semaphore()
    for k in range(1, n_rows):
        pl.semaphore_signal(
            barrier, inc=1, device_id={"rows": lax.rem(me + k, n_rows)}, device_id_type=MESH
        )
    for k in range(1, n_model):
        pl.semaphore_signal(
            barrier, inc=1, device_id={"model": lax.rem(col + k, n_model)}, device_id_type=MESH
        )

    def step(b, rest=()):
        a, start, _ = blocks[b]
        wait_bytes(bufs[a].at[:, :, pl.ds(start, width)], in_sem.at[b])
        if rest:
            for r in rest:
                load(r)
            for n, ref in enumerate((nt_ref, ns_ref)):
                pltpu.make_async_copy(ref, norms.at[n], norm_sem.at[0]).start()

        def one(i, acc):
            rows = pl.ds(pl.multiple_of(i * TILE, TILE), TILE)
            where = (rows, pl.ds(start, width))
            r = adam(*(bufs[a][(k, *where)] for k in range(3)))
            results[a][where] = r
            m = jnp.abs(r).reshape(TILE // 8, 8, width)
            return acc + jnp.sum(m, axis=0)

        acc = lax.fori_loop(0, share // TILE, one, jnp.zeros((8, width), jnp.float32))
        sums[b, me] = jnp.sum(acc, axis=0, keepdims=True)

    def sum_copy(b, k):
        return pltpu.make_async_remote_copy(
            src_ref=sums.at[b, me],
            dst_ref=sums.at[b, me],
            send_sem=sum_send.at[0],
            recv_sem=sum_recv.at[b],
            device_id={"rows": lax.rem(me + k, n_rows)},
            device_id_type=MESH,
        )

    def early_copy(b, n, to):
        a, start, _ = blocks[b]
        return pltpu.make_async_remote_copy(
            src_ref=results[a].at[pl.ds(0, EARLY), pl.ds(start, width)],
            dst_ref=early.at[n],
            send_sem=early_send.at[n],
            recv_sem=early_recv.at[n],
            device_id={"rows": to},
            device_id_type=MESH,
        )

    def gain_model(k):
        return pltpu.make_async_remote_copy(
            src_ref=gains.at[me, col],
            dst_ref=gains.at[me, col],
            send_sem=gain_send.at[0],
            recv_sem=gain_recv.at[0],
            device_id={"model": lax.rem(col + k, n_model)},
            device_id_type=MESH,
        )

    def gain_rows(k):
        return pltpu.make_async_remote_copy(
            src_ref=gains.at[me],
            dst_ref=gains.at[me],
            send_sem=gain_send.at[1],
            recv_sem=gain_recv.at[1],
            device_id={"rows": lax.rem(me + k, n_rows)},
            device_id_type=MESH,
        )

    def work(core):
        now, then = orders[core]
        order = now + then
        gather = Gather(n_rows, share, width, len(now), EARLY, whole, None, sems)
        for i, b in enumerate(order):
            step(b, order[1:] if i == 0 else ())
            if i == 0:
                pl.semaphore_wait(barrier, n_rows + n_model - 2)
            for k in range(1, n_rows):
                sum_copy(b, k).start()
            if i == 0:
                early_copy(b, 0, z * SIDE + other).start()

                @pl.when(z < line - 1)
                def _():
                    early_copy(b, 1, me + SIDE).start()

                @pl.when(z > 0)
                def _():
                    early_copy(b, 2, me - SIDE).start()

        wait_bytes(norms, norm_sem.at[0])
        gains[me, col] = norms[0] + norms[1]
        for k in range(1, n_model):
            gain_model(k).start()

        for i, b in enumerate(order):
            a, start, _ = blocks[b]
            wait_bytes(sums.at[b, pl.ds(0, n_rows - 1)], sum_recv.at[b])
            total = sums[b, 0]
            for k in range(1, n_rows):
                total = total + sums[b, k]
            column = total / d_model
            cols[a][:, pl.ds(start, width)] = column
            scale = jnp.broadcast_to(1.0 / column, (TILE, width))
            mine = i < len(now)
            slot = i if mine else i - len(now)

            def one(t, carry):
                rows = pl.ds(pl.multiple_of(t * TILE, TILE), TILE)
                value = (results[a][rows, pl.ds(start, width)] * scale).astype(jnp.bfloat16)
                where = pl.ds(slot * width, width)
                if mine:
                    whole[pl.ds(pl.multiple_of(me * share + t * TILE, TILE), TILE), where] = value
                else:
                    later[rows, where] = value
                return carry

            lax.fori_loop(0, share // TILE, one, 0)
            if mine:
                gather.send_own(slot)

        a, start, _ = blocks[order[0]]
        scale = jnp.broadcast_to(1.0 / cols[a][:, pl.ds(start, width)], (TILE, width))

        def scaled(n, owner):
            early_copy(order[0], n, owner).wait_recv()

            def one(t, carry):
                rows = pl.ds(pl.multiple_of(t * TILE, TILE), TILE)
                there = pl.ds(pl.multiple_of(owner * share + t * TILE, TILE), TILE)
                whole[there, pl.ds(0, width)] = (early[n, rows] * scale).astype(jnp.bfloat16)
                return carry

            lax.fori_loop(0, EARLY // TILE, one, 0)

        @pl.when(z > 0)
        def _():
            scaled(1, me - SIDE)

        @pl.when(z < line - 1)
        def _():
            scaled(2, me + SIDE)

        scaled(0, z * SIDE + other)

        wait_bytes(gains.at[0, pl.ds(0, n_model - 1)], gain_recv.at[0])
        for k in range(1, n_rows):
            gain_rows(k).start()
        gather.relay()
        early_copy(order[0], 0, me).wait_send()

        @pl.when(z < line - 1)
        def _():
            early_copy(order[0], 1, me).wait_send()

        @pl.when(z > 0)
        def _():
            early_copy(order[0], 2, me).wait_send()

        gather.finish()

    on_core(work)
    wait_bytes(gains.at[pl.ds(0, n_rows - 1)], gain_recv.at[1])
    for r in range(n_rows):
        for m in range(n_model):
            lines[pl.ds(r * n_model + m, 1), :] = gains[r, m]
    norm_out[...] = lines[...].astype(jnp.bfloat16)
    wait_bytes(gains.at[0, pl.ds(0, n_model - 1)], gain_send.at[0])
    wait_bytes(gains.at[pl.ds(0, n_rows - 1)], gain_send.at[1])
    wait_bytes(sums.at[:, pl.ds(0, n_rows - 1)], sum_send.at[0])


def closing(n_rows, blocks, orders, own, token, whole, *sems):
    line = n_rows // SIDE
    me = lax.axis_index("rows")
    z, y = me // SIDE, me % SIDE
    share, width = own.shape[0], blocks[0][2]
    barrier = pltpu.get_barrier_semaphore()

    def signal(who):
        pl.semaphore_signal(barrier, inc=1, device_id={"rows": who}, device_id_type=MESH)

    signal(z * SIDE + 1 - y)

    @pl.when(z > 0)
    def _():
        signal(me - SIDE)

    @pl.when(z < line - 1)
    def _():
        signal(me + SIDE)

    pl.semaphore_wait(barrier, 1 + jnp.where(z > 0, 1, 0) + jnp.where(z < line - 1, 1, 0))

    def work(core):
        count = len(orders[core][1])
        gather = Gather(n_rows, share, width, count, 0, whole, own, sems)
        for slot in range(count):
            gather.send_own(slot)

        def one(t, carry):
            rows = pl.ds(pl.multiple_of(t * TILE, TILE), TILE)
            there = pl.ds(pl.multiple_of(me * share + t * TILE, TILE), TILE)
            whole[there, pl.ds(0, count * width)] = own[rows, pl.ds(0, count * width)]
            return carry

        lax.fori_loop(0, share // TILE, one, 0)
        gather.relay()
        gather.finish()

    on_core(work)


def put(blocks, orders, phase, whole, finals, sem):
    def work(core):
        copies = []
        for slot, b in enumerate(orders[core][phase]):
            a, start, width = blocks[b]
            c = pltpu.make_async_copy(
                whole.at[:, pl.ds(slot * width, width)],
                finals[a].at[:, pl.ds(start, width)],
                sem.at[slot],
            )
            c.start()
            copies.append(c)
        for c in copies:
            c.wait()

    on_core(work)


def write(blocks, orders, *refs):
    whole, small, finals, outs, token, sem = refs[0], refs[1:8], refs[8:11], refs[11:18], refs[18], refs[19]
    most = max(len(o) for c in orders for o in c)
    copies = []
    for n, (src, dst) in enumerate(zip(small, outs)):
        c = pltpu.make_async_copy(src, dst, sem.at[most + n])
        c.start()
        copies.append(c)
    token[...] = jnp.zeros_like(token)
    put(blocks, orders, 0, whole, finals, sem)
    for c in copies:
        c.wait()


def rest(blocks, orders, whole, *refs):
    put(blocks, orders, 1, whole, refs[3:6], refs[6])


def fused(n_rows, n_model, d_model, blocks, arrays):
    *weights, norm_train, norm_step = arrays
    share = weights[0].shape[0]
    widths = [weights[3 * a].shape[1] for a in range(3)]
    line, nb, width = n_rows // SIDE, len(blocks), blocks[0][2]
    unit = norm_train.shape[0]
    big = [b for b in range(nb) if blocks[b][0] == 0]
    few = [b for b in range(nb) if blocks[b][0] != 0]
    orders = ((big, few), (few, big))
    most = max(len(big), len(few))
    anywhere = pl.BlockSpec(memory_space=pl.ANY)
    vmem = pl.BlockSpec(memory_space=pltpu.VMEM)
    f32, b16, dma = jnp.float32, jnp.bfloat16, pltpu.SemaphoreType.DMA
    whole, own, *small = pl.pallas_call(
        functools.partial(opening, n_rows, n_model, blocks, orders, d_model),
        out_shape=[
            pltpu.VMEM((d_model, most * width), b16),
            pltpu.VMEM((share, most * width), b16),
            *(pltpu.VMEM((1, w), f32) for w in widths),
            pltpu.VMEM((n_rows * n_model, unit), b16),
            *(pltpu.VMEM((share, w), f32) for w in widths),
        ],
        in_specs=[anywhere] * 11,
        out_specs=[vmem] * 9,
        scratch_shapes=[
            *(pltpu.VMEM((3, share, w), f32) for w in widths),
            pltpu.VMEM((2, 1, unit), f32),
            pltpu.VMEM((n_rows * n_model, unit), f32),
            pltpu.VMEM((nb, n_rows, 1, width), f32),
            pltpu.VMEM((n_rows, n_model, 1, unit), f32),
            dma((nb,)),
            dma((1,)),
            dma((1,)),
            dma((nb,)),
            dma((2,)),
            dma((2,)),
            pltpu.VMEM((3, EARLY, width), f32),
            dma((3,)),
            dma((3,)),
            *gather_sems(line, most),
        ],
        compiler_params=pltpu.CompilerParams(
            collective_id=0, has_side_effects=True, vmem_limit_bytes=50 * 2**20
        ),
    )(*weights, norm_train.reshape(1, -1), norm_step.reshape(1, -1))
    *finals, c0, c1, c2, serve, r0, r1, r2, token = pl.pallas_call(
        functools.partial(write, blocks, orders),
        out_shape=[
            *(jax.ShapeDtypeStruct((d_model, w), b16) for w in widths),
            *(jax.ShapeDtypeStruct(o.shape, o.dtype) for o in small),
            pltpu.VMEM((8, 128), f32),
        ],
        in_specs=[anywhere] * 8,
        out_specs=[anywhere] * 10 + [vmem],
        scratch_shapes=[dma((most + 7,))],
        compiler_params=pltpu.CompilerParams(vmem_limit_bytes=2**20),
    )(whole, *small)
    whole = pl.pallas_call(
        functools.partial(closing, n_rows, blocks, orders),
        out_shape=pltpu.VMEM((d_model, most * width), b16),
        in_specs=[vmem, anywhere],
        out_specs=vmem,
        scratch_shapes=gather_sems(line, most),
        compiler_params=pltpu.CompilerParams(
            collective_id=1, has_side_effects=True, vmem_limit_bytes=40 * 2**20
        ),
    )(own, token)
    finals = pl.pallas_call(
        functools.partial(rest, blocks, orders),
        out_shape=[jax.ShapeDtypeStruct((d_model, w), b16) for w in widths],
        in_specs=[anywhere] * 4,
        out_specs=[anywhere] * 3,
        scratch_shapes=[dma((most,))],
        input_output_aliases={1: 0, 2: 1, 3: 2},
        compiler_params=pltpu.CompilerParams(vmem_limit_bytes=2**20),
    )(whole, *finals)
    return (*finals, *(d.reshape(-1) for d in (c0, c1, c2, serve)), r0, r1, r2)


def solution(mesh):
    n_rows, n_model = mesh.shape["rows"], mesh.shape["model"]

    def body(*arrays):
        share = arrays[0].shape[0]
        widths = [arrays[3 * a].shape[1] for a in range(3)]
        width = min(widths)
        d_model = share * n_rows
        line = n_rows // SIDE
        counts = (widths[0] // width, (widths[1] + widths[2]) // width)
        fits = (
            n_rows % SIDE == 0
            and n_model % 2 == 0
            and 2 <= line <= 4
            and share % TILE == 0
            and share > EARLY
            and width % 128 == 0
            and all(w % width == 0 for w in widths)
            and all(2 <= c <= 6 and cut_of(line, share, c) < share for c in counts)
        )
        if not fits:
            return plain(d_model, arrays)
        blocks = tuple(
            (a, s, width) for a, w in enumerate(widths) for s in range(0, w, width)
        )
        return fused(n_rows, n_model, d_model, blocks, arrays)

    return jax.shard_map(
        body,
        mesh=mesh,
        in_specs=(P("rows", "model"),) * 9 + (P(("rows", "model")),) * 2,
        out_specs=(
            *(P(None, "model"),) * 3,
            *(P("model"),) * 3,
            P(),
            *(P("rows", "model"),) * 3,
        ),
        check_vma=False,
    )
```

time: 137 us -> 133 us (0.971)
  Pallas kernels: 136 us -> 132 us
    pallas_call x2 -> x4, Pallas kernels: 136 us -> 132 us  [the longest x1 79.4 us: fused(): pl.pallas_call(functools.partial(opening, n_rows, n_model, blocks, orders...]
where the time goes in v3:
time: 133 us
  Pallas kernels  132 us (99%)
    pallas_call x1, Pallas kernels, fused(): pl.pallas_call(functools.partial(opening, n_rows, n_model, blocks, orders...  79.4 us
    pallas_call x1, Pallas kernels, fused(): pl.pallas_call(functools.partial(closing, n_rows, blocks, orders), out_sh...  46.2 us
    pallas_call x1, Pallas kernels, fused(): pl.pallas_call(functools.partial(write, blocks, orders), out_shape=[*(jax...  4.44 us

profile of v3, /device:TPU:0, one launch (start us, length us, event | category | flops | bytes accessed | tf_op | source)
XLA Modules:
  0.0 132.8 jit_solution(8074067444206078272)
XLA Ops:
  0.6 79.4 %shard_map.186 = (bf16[4096,1024]{1,0:T(8,128)(2,1)S(1)}, bf16[512,1024]{1,0:T(8,128)(2,1)S(1)}, f32[1,1024]{1,0:T(1,128)S(1)}, f32[1,256]{1,0:T(1,128)S(1)}, f3...) custom-call(f32[512,1024]{1,0:T(8,128)} %refs_0_.1, ...), custom_call_target="tpu_custom_call" | custom-call | tf_op jit(solution)/shard_map/pallas_call | solution.py:487
  80.1 4.4 %shard_map.187 = (bf16[4096,1024]{1,0:T(8,128)(2,1)}, bf16[4096,256]{1,0:T(8,128)(2,1)}, bf16[4096,256]{1,0:T(8,128)(2,1)}, f32[1,1024]{1,0:T(1,128)}, f32[1,256...) custom-call(bf16[4096,1024]{1,0:T(8,128)(2,1)S(1)} %get-tuple-elemen, ...), custom_call_target="tpu_custom_call" | custom-call | tf_op jit(solution)/shard_map/pallas_call | solution.py:519
  84.5 46.2 %shard_map.188.whole = bf16[4096,1024]{1,0:T(8,128)(2,1)S(1)} custom-call(bf16[512,1024]{1,0:T(8,128)(2,1)S(1)} %get-tuple-element.33.own, f32[8,128]{1,0:T(8,128)S(1)} %get-tuple-element.42.token), custom_call_target="tpu_custom_call" | custom-call | tf_op jit(solution)/shard_map/pallas_call | solution.py:531
  130.8 2.1 %shard_map.189 = (bf16[4096,1024]{1,0:T(8,128)(2,1)}, bf16[4096,256]{1,0:T(8,128)(2,1)}, bf16[4096,256]{1,0:T(8,128)(2,1)}) custom-call(bf16[4096,1024]{1,0:T(8,128)(2,1)S(1)} %shard_map.188.whole, bf16[4096,1024]{1,0:T(8,128)(2,1)} %get-tuple-element.43.refs_0_, ...), custom_call_target="tpu_custom_call", output_to_operand_aliasing={{0}: (1, {}), {1}: (2, {}), {2}: (3, {})} | custom-call | tf_op jit(solution)/shard_map/pallas_call | solution.py:541

commit v4 on v3

--- a/solution.py
+++ b/solution.py
@@ -14,8 +14,7 @@
 MESH = pl.DeviceIdType.MESH
 SIDE = 2
 TILE = 32
-EARLY = 128
-PAIR = 1
+EARLY = (128, 128)
 
 
 def adam(w, first, second):
@@ -57,8 +56,14 @@
         self.z, self.y = self.me // SIDE, self.me % SIDE
         self.cut = cut_of(self.line, share, count)
         cut = self.cut
-        self.chunks = [(j, 0, share, False) for j in range(count) if j != PAIR]
-        self.chunks += [(PAIR, cut, share, False), (PAIR, 0, cut, False), (PAIR, 0, cut, True)]
+        self.pair = pair = min(1, count - 1)
+        full = [(j, 0, share, False) for j in range(count) if j != pair]
+        head = [(pair, cut, share, False)]
+        if own is not None:
+            slot, first, last, _ = (full or head).pop()
+            mid = (first + last) // 64 * 32
+            head += [(slot, first, mid, False), (slot, mid, last, False)]
+        self.chunks = full + head + [(pair, 0, cut, False), (pair, 0, cut, True)]
         self.spread = len(self.chunks) - 2
 
     def part(self, slot, owner, first, last, ref=None):
@@ -74,7 +79,7 @@
     def to_line(self, zs, c, up, to, near=False, mine=False):
         slot, first, last, crossed = self.chunks[c]
         if near and slot == 0:
-            first = self.skip
+            first = max(first, self.skip)
         owner = zs * SIDE + (1 - self.y if crossed else self.y)
         there = self.part(slot, owner, first, last)
         here = there
@@ -90,11 +95,12 @@
             device_id_type=MESH,
         )
 
-    def to_side(self, zs, slot, first, from_me=True, mine=False):
+    def to_side(self, zs, slot, first, from_me=True, mine=False, last=None):
         owner = zs * SIDE + (self.y if from_me else 1 - self.y)
-        there = self.part(slot, owner, first, self.share)
-        here = self.part(slot, owner, first, self.share, self.own) if mine else there
-        group = self.line if mine and slot == PAIR else zs
+        last = self.share if last is None else last
+        there = self.part(slot, owner, first, last)
+        here = self.part(slot, owner, first, last, self.own) if mine else there
+        group = self.line if mine and slot == self.pair else zs
         return pltpu.make_async_remote_copy(
             src_ref=here,
             dst_ref=there,
@@ -121,34 +127,42 @@
                 self.both_ways(c)
         self.to_side(self.z, slot, self.skip if slot == 0 else 0, mine=True).start()
 
+    def pass_on(self, d, c):
+        z, line = self.z, self.line
+        slot, first, last, _ = self.chunks[c]
+
+        @pl.when(z - d >= 0)
+        def _():
+            self.to_line(z - d, c, True, z, d == 1).wait_recv()
+
+            @pl.when(z < line - 1)
+            def _():
+                self.to_line(z - d, c, True, z + 1).start()
+
+            if c < self.spread:
+                self.to_side(z - d, slot, first, last=last).start()
+
+        @pl.when(z + d < line)
+        def _():
+            self.to_line(z + d, c, False, z, d == 1).wait_recv()
+
+            @pl.when(z > 0)
+            def _():
+                self.to_line(z + d, c, False, z - 1).start()
+
+            if c < self.spread:
+                self.to_side(z + d, slot, first, last=last).start()
+
     def relay(self):
-        z, line = self.z, self.line
-        self.to_side(z, PAIR, 0, False, True).wait_recv()
-        self.both_ways(len(self.chunks) - 1)
-        for d in range(1, line):
-            for c, (slot, first, _, _) in enumerate(self.chunks):
-
-                @pl.when(z - d >= 0)
-                def _():
-                    self.to_line(z - d, c, True, z, d == 1).wait_recv()
-
-                    @pl.when(z < line - 1)
-                    def _():
-                        self.to_line(z - d, c, True, z + 1).start()
-
-                    if c < self.spread:
-                        self.to_side(z - d, slot, first).start()
-
-                @pl.when(z + d < line)
-                def _():
-                    self.to_line(z + d, c, False, z, d == 1).wait_recv()
-
-                    @pl.when(z > 0)
-                    def _():
-                        self.to_line(z + d, c, False, z - 1).start()
-
-                    if c < self.spread:
-                        self.to_side(z + d, slot, first).start()
+        crossed = len(self.chunks) - 1
+        for d in range(1, self.line):
+            for c in range(crossed):
+                self.pass_on(d, c)
+            if d == 1:
+                self.to_side(self.z, self.pair, 0, False, True).wait_recv()
+                self.both_ways(crossed)
+        for d in range(1, self.line):
+            self.pass_on(d, crossed)
 
     def finish(self):
         z, line, share, count, cut = self.z, self.line, self.share, self.count, self.cut
@@ -162,7 +176,7 @@
         def _():
             wait_bytes(self.some(full - self.skip), self.own_send.at[1])
 
-        self.to_side(z, PAIR, 0, mine=True).wait_send()
+        self.to_side(z, self.pair, 0, mine=True).wait_send()
         for zs in range(line):
 
             @pl.when((z > 0) & (z < zs))
@@ -175,9 +189,11 @@
 
             for sem in (self.side_recv, self.side_send):
 
-                @pl.when(z == zs)
-                def _():
-                    wait_bytes(self.some((count - 1) * share - self.skip), sem.at[zs])
+                if count > 1:
+
+                    @pl.when(z == zs)
+                    def _():
+                        wait_bytes(self.some((count - 1) * share - self.skip), sem.at[zs])
 
                 @pl.when(z != zs)
                 def _():
@@ -191,7 +207,7 @@
 def gather_sems(line, most):
     dma = pltpu.SemaphoreType.DMA
     return [dma((2,)), dma((line,)), dma((line,)), dma((line + 1,)),
-            dma((line - 1, most + 2)), dma((line + 1,))]
+            dma((line - 1, most + 3)), dma((line + 1,))]
 
 
 def opening(n_rows, n_model, blocks, orders, d_model, *refs):
@@ -260,11 +276,11 @@
             device_id_type=MESH,
         )
 
-    def early_copy(b, n, to):
+    def early_copy(b, n, to, rows):
         a, start, _ = blocks[b]
         return pltpu.make_async_remote_copy(
-            src_ref=results[a].at[pl.ds(0, EARLY), pl.ds(start, width)],
-            dst_ref=early.at[n],
+            src_ref=results[a].at[pl.ds(0, rows), pl.ds(start, width)],
+            dst_ref=early.at[n, pl.ds(0, rows)],
             send_sem=early_send.at[n],
             recv_sem=early_recv.at[n],
             device_id={"rows": to},
@@ -294,23 +310,24 @@
     def work(core):
         now, then = orders[core]
         order = now + then
-        gather = Gather(n_rows, share, width, len(now), EARLY, whole, None, sems)
+        ahead = EARLY[core]
+        gather = Gather(n_rows, share, width, len(now), ahead, whole, None, sems)
         for i, b in enumerate(order):
             step(b, order[1:] if i == 0 else ())
             if i == 0:
                 pl.semaphore_wait(barrier, n_rows + n_model - 2)
             for k in range(1, n_rows):
                 sum_copy(b, k).start()
-            if i == 0:
-                early_copy(b, 0, z * SIDE + other).start()
+            if i == 0 and ahead:
+                early_copy(b, 0, z * SIDE + other, ahead).start()
 
                 @pl.when(z < line - 1)
                 def _():
-                    early_copy(b, 1, me + SIDE).start()
+                    early_copy(b, 1, me + SIDE, ahead).start()
 
                 @pl.when(z > 0)
                 def _():
-                    early_copy(b, 2, me - SIDE).start()
+                    early_copy(b, 2, me - SIDE, ahead).start()
 
         wait_bytes(norms, norm_sem.at[0])
         gains[me, col] = norms[0] + norms[1]
@@ -343,43 +360,45 @@
             if mine:
                 gather.send_own(slot)
 
-        a, start, _ = blocks[order[0]]
-        scale = jnp.broadcast_to(1.0 / cols[a][:, pl.ds(start, width)], (TILE, width))
-
-        def scaled(n, owner):
-            early_copy(order[0], n, owner).wait_recv()
-
-            def one(t, carry):
-                rows = pl.ds(pl.multiple_of(t * TILE, TILE), TILE)
-                there = pl.ds(pl.multiple_of(owner * share + t * TILE, TILE), TILE)
-                whole[there, pl.ds(0, width)] = (early[n, rows] * scale).astype(jnp.bfloat16)
-                return carry
-
-            lax.fori_loop(0, EARLY // TILE, one, 0)
-
-        @pl.when(z > 0)
-        def _():
-            scaled(1, me - SIDE)
-
-        @pl.when(z < line - 1)
-        def _():
-            scaled(2, me + SIDE)
-
-        scaled(0, z * SIDE + other)
+        if ahead:
+            a, start, _ = blocks[order[0]]
+            scale = jnp.broadcast_to(1.0 / cols[a][:, pl.ds(start, width)], (TILE, width))
+
+            def scaled(n, owner):
+                early_copy(order[0], n, owner, ahead).wait_recv()
+
+                def one(t, carry):
+                    rows = pl.ds(pl.multiple_of(t * TILE, TILE), TILE)
+                    there = pl.ds(pl.multiple_of(owner * share + t * TILE, TILE), TILE)
+                    whole[there, pl.ds(0, width)] = (early[n, rows] * scale).astype(jnp.bfloat16)
+                    return carry
+
+                lax.fori_loop(0, ahead // TILE, one, 0)
+
+            @pl.when(z > 0)
+            def _():
+                scaled(1, me - SIDE)
+
+            @pl.when(z < line - 1)
+            def _():
+                scaled(2, me + SIDE)
+
+            scaled(0, z * SIDE + other)
 
         wait_bytes(gains.at[0, pl.ds(0, n_model - 1)], gain_recv.at[0])
         for k in range(1, n_rows):
             gain_rows(k).start()
         gather.relay()
-        early_copy(order[0], 0, me).wait_send()
-
-        @pl.when(z < line - 1)
-        def _():
-            early_copy(order[0], 1, me).wait_send()
-
-        @pl.when(z > 0)
-        def _():
-            early_copy(order[0], 2, me).wait_send()
+        if ahead:
+            early_copy(order[0], 0, me, ahead).wait_send()
+
+            @pl.when(z < line - 1)
+            def _():
+                early_copy(order[0], 1, me, ahead).wait_send()
+
+            @pl.when(z > 0)
+            def _():
+                early_copy(order[0], 2, me, ahead).wait_send()
 
         gather.finish()
 
@@ -480,15 +499,15 @@
     big = [b for b in range(nb) if blocks[b][0] == 0]
     few = [b for b in range(nb) if blocks[b][0] != 0]
     orders = ((big, few), (few, big))
-    most = max(len(big), len(few))
+    most = [max(len(orders[c][p]) for c in range(2)) for p in range(2)]
     anywhere = pl.BlockSpec(memory_space=pl.ANY)
     vmem = pl.BlockSpec(memory_space=pltpu.VMEM)
     f32, b16, dma = jnp.float32, jnp.bfloat16, pltpu.SemaphoreType.DMA
     whole, own, *small = pl.pallas_call(
         functools.partial(opening, n_rows, n_model, blocks, orders, d_model),
         out_shape=[
-            pltpu.VMEM((d_model, most * width), b16),
-            pltpu.VMEM((share, most * width), b16),
+            pltpu.VMEM((d_model, most[0] * width), b16),
+            pltpu.VMEM((share, most[1] * width), b16),
             *(pltpu.VMEM((1, w), f32) for w in widths),
             pltpu.VMEM((n_rows * n_model, unit), b16),
             *(pltpu.VMEM((share, w), f32) for w in widths),
@@ -507,13 +526,13 @@
             dma((nb,)),
             dma((2,)),
             dma((2,)),
-            pltpu.VMEM((3, EARLY, width), f32),
+            pltpu.VMEM((3, max(EARLY), width), f32),
             dma((3,)),
             dma((3,)),
-            *gather_sems(line, most),
+            *gather_sems(line, most[0]),
         ],
         compiler_params=pltpu.CompilerParams(
-            collective_id=0, has_side_effects=True, vmem_limit_bytes=50 * 2**20
+            collective_id=0, has_side_effects=True, vmem_limit_bytes=49 * 2**20
         ),
     )(*weights, norm_train.reshape(1, -1), norm_step.reshape(1, -1))
     *finals, c0, c1, c2, serve, r0, r1, r2, token = pl.pallas_call(
@@ -525,15 +544,15 @@
         ],
         in_specs=[anywhere] * 8,
         out_specs=[anywhere] * 10 + [vmem],
-        scratch_shapes=[dma((most + 7,))],
+        scratch_shapes=[dma((max(most) + 7,))],
         compiler_params=pltpu.CompilerParams(vmem_limit_bytes=2**20),
     )(whole, *small)
     whole = pl.pallas_call(
         functools.partial(closing, n_rows, blocks, orders),
-        out_shape=pltpu.VMEM((d_model, most * width), b16),
+        out_shape=pltpu.VMEM((d_model, most[1] * width), b16),
         in_specs=[vmem, anywhere],
         out_specs=vmem,
-        scratch_shapes=gather_sems(line, most),
+        scratch_shapes=gather_sems(line, most[1]),
         compiler_params=pltpu.CompilerParams(
             collective_id=1, has_side_effects=True, vmem_limit_bytes=40 * 2**20
         ),
@@ -543,7 +562,7 @@
         out_shape=[jax.ShapeDtypeStruct((d_model, w), b16) for w in widths],
         in_specs=[anywhere] * 4,
         out_specs=[anywhere] * 3,
-        scratch_shapes=[dma((most,))],
+        scratch_shapes=[dma((most[1],))],
         input_output_aliases={1: 0, 2: 1, 3: 2},
         compiler_params=pltpu.CompilerParams(vmem_limit_bytes=2**20),
     )(whole, *finals)
@@ -559,16 +578,17 @@
         width = min(widths)
         d_model = share * n_rows
         line = n_rows // SIDE
-        counts = (widths[0] // width, (widths[1] + widths[2]) // width)
+        counts = (1, widths[0] // width, (widths[0] + widths[1] + widths[2]) // width - 1)
         fits = (
             n_rows % SIDE == 0
             and n_model % 2 == 0
             and 2 <= line <= 4
-            and share % TILE == 0
-            and share > EARLY
+            and share % (2 * TILE) == 0
+            and share > max(EARLY)
             and width % 128 == 0
             and all(w % width == 0 for w in widths)
-            and all(2 <= c <= 6 and cut_of(line, share, c) < share for c in counts)
+            and counts[1] > 1
+            and all(cut_of(line, share, c) <= share - 64 for c in counts)
         )
         if not fits:
             return plain(d_model, arrays)

time: 133 us -> 131 us (0.985)
  Pallas kernels: 132 us -> 130 us
    pallas_call x1, Pallas kernels: 46.2 us -> 41.1 us  [fused(): pl.pallas_call(functools.partial(closing, n_rows, blocks, orders), out_sh...]
    pallas_call x1, Pallas kernels: 79.4 us -> 82.4 us  [fused(): pl.pallas_call(functools.partial(opening, n_rows, n_model, blocks, orders...]
where the time goes in v4:
time: 131 us
  Pallas kernels  130 us (99%)
    pallas_call x1, Pallas kernels, fused(): pl.pallas_call(functools.partial(opening, n_rows, n_model, blocks, orders...  82.4 us
    pallas_call x1, Pallas kernels, fused(): pl.pallas_call(functools.partial(closing, n_rows, blocks, orders), out_sh...  41.1 us
    pallas_call x1, Pallas kernels, fused(): pl.pallas_call(functools.partial(write, blocks, orders), out_shape=[*(jax...  4.44 us

profile of v4, /device:TPU:0, one launch (start us, length us, event | category | flops | bytes accessed | tf_op | source)
XLA Modules:
  0.0 130.6 jit_solution(6423898689603067657)
XLA Ops:
  0.6 82.4 %shard_map.186 = (bf16[4096,1024]{1,0:T(8,128)(2,1)S(1)}, bf16[512,1024]{1,0:T(8,128)(2,1)S(1)}, f32[1,1024]{1,0:T(1,128)S(1)}, f32[1,256]{1,0:T(1,128)S(1)}, f3...) custom-call(f32[512,1024]{1,0:T(8,128)} %refs_0_.1, ...), custom_call_target="tpu_custom_call" | custom-call | tf_op jit(solution)/shard_map/pallas_call | solution.py:506
  83.0 4.4 %shard_map.187 = (bf16[4096,1024]{1,0:T(8,128)(2,1)}, bf16[4096,256]{1,0:T(8,128)(2,1)}, bf16[4096,256]{1,0:T(8,128)(2,1)}, f32[1,1024]{1,0:T(1,128)}, f32[1,256...) custom-call(bf16[4096,1024]{1,0:T(8,128)(2,1)S(1)} %get-tuple-elemen, ...), custom_call_target="tpu_custom_call" | custom-call | tf_op jit(solution)/shard_map/pallas_call | solution.py:538
  87.5 41.1 %shard_map.188.whole = bf16[4096,1024]{1,0:T(8,128)(2,1)S(1)} custom-call(bf16[512,1024]{1,0:T(8,128)(2,1)S(1)} %get-tuple-element.33.own, f32[8,128]{1,0:T(8,128)S(1)} %get-tuple-element.42.token), custom_call_target="tpu_custom_call" | custom-call | tf_op jit(solution)/shard_map/pallas_call | solution.py:550
  128.5 2.1 %shard_map.189 = (bf16[4096,1024]{1,0:T(8,128)(2,1)}, bf16[4096,256]{1,0:T(8,128)(2,1)}, bf16[4096,256]{1,0:T(8,128)(2,1)}) custom-call(bf16[4096,1024]{1,0:T(8,128)(2,1)S(1)} %shard_map.188.whole, bf16[4096,1024]{1,0:T(8,128)(2,1)} %get-tuple-element.43.refs_0_, ...), custom_call_target="tpu_custom_call", output_to_operand_aliasing={{0}: (1, {}), {1}: (2, {}), {2}: (3, {})} | custom-call | tf_op jit(solution)/shard_map/pallas_call | solution.py:560

commit v5 on v4

--- a/solution.py
+++ b/solution.py
@@ -227,15 +227,24 @@
     share = bufs[0].shape[1]
     width = blocks[0][2]
 
-    def load(b):
+    half = share // 2
+
+    def load(b, rows=pl.ds(0, share), sem=None):
         a, start, _ = blocks[b]
-        where = (slice(None), pl.ds(start, width))
+        where = (rows, pl.ds(start, width))
         for k in range(3):
             pltpu.make_async_copy(
-                ins[3 * a + k].at[where], bufs[a].at[(k, *where)], in_sem.at[b]
+                ins[3 * a + k].at[where],
+                bufs[a].at[(k, *where)],
+                in_sem.at[b if sem is None else sem],
             ).start()
 
-    on_core(lambda c: load(orders[c][0][0]))
+    def load_first(core):
+        b = orders[core][0][0]
+        load(b, pl.ds(0, half), len(blocks))
+        load(b, pl.ds(half, half))
+
+    on_core(load_first)
     barrier = pltpu.get_barrier_semaphore()
     for k in range(1, n_rows):
         pl.semaphore_signal(
@@ -248,13 +257,6 @@
 
     def step(b, rest=()):
         a, start, _ = blocks[b]
-        wait_bytes(bufs[a].at[:, :, pl.ds(start, width)], in_sem.at[b])
-        if rest:
-            for r in rest:
-                load(r)
-            for n, ref in enumerate((nt_ref, ns_ref)):
-                pltpu.make_async_copy(ref, norms.at[n], norm_sem.at[0]).start()
-
         def one(i, acc):
             rows = pl.ds(pl.multiple_of(i * TILE, TILE), TILE)
             where = (rows, pl.ds(start, width))
@@ -263,7 +265,21 @@
             m = jnp.abs(r).reshape(TILE // 8, 8, width)
             return acc + jnp.sum(m, axis=0)
 
-        acc = lax.fori_loop(0, share // TILE, one, jnp.zeros((8, width), jnp.float32))
+        acc, done = jnp.zeros((8, width), jnp.float32), 0
+        if rest:
+            wait_bytes(bufs[a].at[:, pl.ds(0, half), pl.ds(start, width)], in_sem.at[len(blocks)])
+            done = half
+            acc = lax.fori_loop(0, done // TILE, one, acc)
+        wait_bytes(
+            bufs[a].at[:, pl.ds(done, share - done), pl.ds(start, width)], in_sem.at[b]
+        )
+        if rest:
+            for r in rest:
+                load(r)
+            for n, ref in enumerate((nt_ref, ns_ref)):
+                pltpu.make_async_copy(ref, norms.at[n], norm_sem.at[0]).start()
+
+        acc = lax.fori_loop(done // TILE, share // TILE, one, acc)
         sums[b, me] = jnp.sum(acc, axis=0, keepdims=True)
 
     def sum_copy(b, k):
@@ -520,7 +536,7 @@
             pltpu.VMEM((n_rows * n_model, unit), f32),
             pltpu.VMEM((nb, n_rows, 1, width), f32),
             pltpu.VMEM((n_rows, n_model, 1, unit), f32),
-            dma((nb,)),
+            dma((nb + 1,)),
             dma((1,)),
             dma((1,)),
             dma((nb,)),

time: 131 us -> 131 us (level)
  no operation moved by 1% of the time
where the time goes in v5:
time: 131 us
  Pallas kernels  130 us (99%)
    pallas_call x1, Pallas kernels, fused(): pl.pallas_call(functools.partial(opening, n_rows, n_model, blocks, orders...  81.9 us
    pallas_call x1, Pallas kernels, fused(): pl.pallas_call(functools.partial(closing, n_rows, blocks, orders), out_sh...  41.6 us
    pallas_call x1, Pallas kernels, fused(): pl.pallas_call(functools.partial(write, blocks, orders), out_shape=[*(jax...  4.44 us

profile of v5, /device:TPU:0, one launch (start us, length us, event | category | flops | bytes accessed | tf_op | source)
XLA Modules:
  0.0 130.6 jit_solution(15677170833805358106)
XLA Ops:
  0.6 81.9 %shard_map.186 = (bf16[4096,1024]{1,0:T(8,128)(2,1)S(1)}, bf16[512,1024]{1,0:T(8,128)(2,1)S(1)}, f32[1,1024]{1,0:T(1,128)S(1)}, f32[1,256]{1,0:T(1,128)S(1)}, f3...) custom-call(f32[512,1024]{1,0:T(8,128)} %refs_0_.1, ...), custom_call_target="tpu_custom_call" | custom-call | tf_op jit(solution)/shard_map/pallas_call | solution.py:522
  82.5 4.4 %shard_map.187 = (bf16[4096,1024]{1,0:T(8,128)(2,1)}, bf16[4096,256]{1,0:T(8,128)(2,1)}, bf16[4096,256]{1,0:T(8,128)(2,1)}, f32[1,1024]{1,0:T(1,128)}, f32[1,256...) custom-call(bf16[4096,1024]{1,0:T(8,128)(2,1)S(1)} %get-tuple-elemen, ...), custom_call_target="tpu_custom_call" | custom-call | tf_op jit(solution)/shard_map/pallas_call | solution.py:554
  87.0 41.6 %shard_map.188.whole = bf16[4096,1024]{1,0:T(8,128)(2,1)S(1)} custom-call(bf16[512,1024]{1,0:T(8,128)(2,1)S(1)} %get-tuple-element.33.own, f32[8,128]{1,0:T(8,128)S(1)} %get-tuple-element.42.token), custom_call_target="tpu_custom_call" | custom-call | tf_op jit(solution)/shard_map/pallas_call | solution.py:566
  128.5 2.1 %shard_map.189 = (bf16[4096,1024]{1,0:T(8,128)(2,1)}, bf16[4096,256]{1,0:T(8,128)(2,1)}, bf16[4096,256]{1,0:T(8,128)(2,1)}) custom-call(bf16[4096,1024]{1,0:T(8,128)(2,1)S(1)} %shard_map.188.whole, bf16[4096,1024]{1,0:T(8,128)(2,1)} %get-tuple-element.43.refs_0_, ...), custom_call_target="tpu_custom_call", output_to_operand_aliasing={{0}: (1, {}), {1}: (2, {}), {2}: (3, {})} | custom-call | tf_op jit(solution)/shard_map/pallas_call | solution.py:576
